TPU v7x, 32 devices: a whole 2x2x4 slice. The times are simulated.
32 devices in a mesh: grp: 4 (over y, x), brick: 8 (over z, core).
Axes of the slice: x: 2, y: 2, z: 4, core: 2. Of those that a mesh axis runs over, the one named last changes fastest.
Arguments:
- coeffs: bfloat16 [8, 4096, 1024], P(None, 'brick'), may hold values from -6 to 6
- tensor: bfloat16 [32, 1024, 1024], P('grp', 'brick'), may hold values from -0.005859375 to 0.005859375
- pairs: int32 [2, 2], replicated, may hold values from 0 to 7
- lateral: int32 [4096], P('brick'), may hold values from 0 to 511
- thermal: float32 [8], replicated, may hold values from 0.5 to 1
Outputs:
- updated: float32 [32, 8, 4096], P(None, None, 'brick')
Inputs may be any that keep to these rules, and one draw needn't show every extreme that they name: `pairs`: row p names the species that receives the collision term and the species it collides with. A cell's lateral partner, as an index within the same block of 512 cells.
All inputs are finite; a program needn't handle non-finite values.
Results may differ from a plain program's by a relative error of at most 0.0003.
Values may be sent and summed in bfloat16 or wider, within the bound.
A program may use at most 128 MiB of HBM per device.

v0:
```python
import jax
import jax.numpy as jnp
from jax import lax
from jax.sharding import PartitionSpec as P

PLANE = 128
collision_update = 0.5
courant = 0.08
max_speed = 11.0
mixing = 0.2


def with_halo(cells, sides, width):
    for axis, dim in sides:
        count = lax.axis_size(axis)
        head = lax.slice_in_dim(cells, 0, width, axis=dim)
        tail = lax.slice_in_dim(cells, cells.shape[dim] - width, cells.shape[dim], axis=dim)
        cells = jnp.concatenate(
            [
                lax.ppermute(tail, axis, [(i, (i + 1) % count) for i in range(count)]),
                cells,
                lax.ppermute(head, axis, [((i + 1) % count, i) for i in range(count)]),
            ],
            axis=dim,
        )
    return cells


def advance(extended, thermal, partner):
    mode_count = extended.shape[0] - 2
    thermo = thermal[None, :, None, None]
    orders = jnp.arange(mode_count, dtype=jnp.int32).astype(jnp.float32)[:, None, None, None]
    speed = thermo * (
        jnp.sqrt(orders) * extended[:mode_count] + jnp.sqrt(orders + 1.0) * extended[2:]
    )
    middle = extended[1 : mode_count + 1]
    face = 0.5 * (speed[:, :, :-1] + speed[:, :, 1:]) - 0.5 * max_speed * thermo * (
        middle[:, :, 1:] - middle[:, :, :-1]
    )
    center = middle[:, :, 1:-1]
    shape_flat = (mode_count, center.shape[1], center.shape[2] * center.shape[3])
    center = center.reshape(shape_flat)
    divergence = (face[:, :, 1:] - face[:, :, :-1]).reshape(shape_flat)
    beside = jnp.take(center, partner, axis=2)
    return center - courant * divergence + mixing * (beside - center)


def local(coeffs, tensor, pairs, lateral, thermal):
    species, cells, width = coeffs.shape
    local_modes = tensor.shape[0]
    group_count = lax.axis_size("grp")
    modes = local_modes * group_count
    pair_count = pairs.shape[0]
    layers = cells // PLANE
    left_rows = jnp.transpose(coeffs[pairs[:, 0]], (2, 0, 1))
    right_flat = coeffs[pairs[:, 1]].reshape(pair_count * cells, width)
    brick_window = jnp.transpose(coeffs[:, :, :modes], (2, 0, 1))
    padded_state = jnp.pad(brick_window, ((1, 1), (0, 0), (0, 0)))
    indicator_matrix = (
        pairs[:, 0][:, None] == jnp.arange(species, dtype=jnp.int32)[None, :]
    ).astype(jnp.float32)
    piece = lax.all_gather(tensor, "brick", axis=1, tiled=True)
    rows_here = piece.shape[1]
    inner = lax.dot_general(
        piece.reshape(local_modes * rows_here, width),
        right_flat,
        (((1,), (1,)), ((), ())),
        preferred_element_type=jnp.float32,
    )
    inner = inner.reshape(local_modes, rows_here, pair_count, cells)
    factor = left_rows.astype(jnp.float32)
    collide = jnp.sum(inner * factor[None], axis=1)
    pair_all = lax.all_gather(collide, "grp", axis=0, tiled=True)
    pair_extended = jnp.pad(pair_all, ((1, 1), (0, 0), (0, 0)))
    span = pair_extended.shape[0]
    collision_extended = jnp.einsum(
        "quw,ut->qtw", pair_extended, indicator_matrix, precision=lax.Precision.HIGHEST
    )
    species_state = padded_state.astype(jnp.float32) + collision_update * collision_extended
    extended = with_halo(species_state.reshape(span, species, layers, PLANE), (("brick", 2),), 1)
    updated = advance(extended, thermal, lateral)
    return updated


def solution(mesh):
    in_specs = (P(None, "brick", None), P("grp", "brick", None), P(), P("brick"), P())
    out_specs = P(None, None, "brick")
    return jax.shard_map(local, mesh=mesh, in_specs=in_specs, out_specs=out_specs, check_vma=False)
```

profile of v0, /device:TPU:0, one launch (start us, length us, event | category | flops | bytes accessed | tf_op | source)
XLA Modules:
  0.0 258.7 jit_solution(1344560839948286816)
XLA Ops:
  6.5 0.0 copy-start.2
  6.5 0.0 all-gather.2.cloned.1.call-start
  6.5 0.7 all-gather.2.cloned.1.call-update
  7.3 0.0 copy-done.2
  7.3 0.2 slice_reduce_fusion
  7.5 0.0 slice-start
  7.5 0.0 copy-start.3
  7.5 0.0 copy-start.1
  7.5 5.5 %gather_fusion = bf16[2,512,1024]{2,1,0:T(8,128)(2,1)} fusion(bf16[8,512,1024]{2,1,0:T(8,128)(2,1)} %param.5, s32[1024]{0:T(1024)S(1)} %get-tuple-element.11), kind=kCustom, calls=%fused_computation | custom fusion | bytes 4194312 | tf_op jit(solution)/shard_map/gather | solution.py:56
  13.0 4.1 %gather_fusion.1 = bf16[2,512,1024]{2,1,0:T(8,128)(2,1)S(1)} fusion(bf16[8,512,1024]{2,1,0:T(8,128)(2,1)} %param.5, s32[1024]{0:T(1024)S(1)} %get-tuple-element.10), kind=kCustom, calls=%fused_computation.1 | custom fusion | bytes 4194312 | tf_op jit(solution)/shard_map/gather | solution.py:55
  17.0 0.0 slice-done
  17.0 1.2 copy.14
  18.3 0.0 copy-done.3
  18.3 0.0 copy-done.1
  18.3 2.6 convert_bitcast_fusion
  20.9 141.9 %all-gather.2.cloned.1.call-done = bf16[8,1024,1024]{2,1,0:T(8,128)(2,1)} async-done(((bf16[8,128,1024]{2,1,0:T(8,128)(2,1)}), bf16[8,1024,1024]{2,1,0:T(8,128)(2,1)}) %all-gather.2.cloned.1.call-update) | async-done | bytes 16777232 | tf_op jit(solution)/shard_map/all_gather | solution.py:62
  162.8 25.8 %fusion.22 = f32[1024,8192]{1,0:T(8,128)} fusion(bf16[1024,1024]{1,0:T(8,128)(2,1)} %bitcast.38, bf16[8192,1024]{1,0:T(8,128)(2,1)} %bitcast.40), kind=kOutput, calls=%fused_computation.47 | convolution fusion | flops 17179869184 | bytes 52428800 | tf_op jit(solution)/shard_map/dot_general | solution.py:64
  188.6 0.0 copy-start
  188.6 37.4 %copy.15 = f32[128,8,8,1024]{3,2,1,0:T(8,128)S(1)} copy(f32[128,8,8,1024]{3,1,2,0:T(8,128)} %bitcast.34) | data formatting | bytes 67108864
  226.0 0.0 copy-done
  226.0 3.9 %multiply_reduce_fusion = f32[8,2,512]{0,2,1:T(8,128)S(1)} fusion(f32[8,1024,2,512]{1,0,3,2:T(8,128)S(1)} %bitcast.33, f32[1024,2,512]{0,2,1:T(8,128)S(1)} %copy-done), kind=kLoop, calls=%fused_computation.3 | loop fusion | flops 16769024 | bytes 37781504 | tf_op jit(solution)/shard_map/reduce_sum | solution.py:72
  230.0 0.2 copy.11
  230.1 8.4 %all_gather.7 = f32[32,2,512]{2,1,0:T(2,128)S(1)} all-gather(f32[8,2,512]{2,1,0:T(2,128)S(1)} %copy.11), channel_id=1, replica_groups=mesh['grp'=4,'brick'=8] {'grp'}, dimensions={0}, use_global_device_ids=true | all-gather | bytes 163840 | tf_op jit(solution)/shard_map/all_gather | solution.py:73
  238.6 1.5 fusion.1
  240.0 0.7 fusion.21
  240.8 0.0 collective-permute-start
  240.8 3.5 %collective-permute-start.1 = (f32[34,8,1,128]{3,1,2,0:T(8,128)}, f32[34,8,1,128]{3,1,2,0:T(8,128)S(1)}, u32[]{:S(2)}, u32[]{:S(2)}) collective-permute-start(f32[34,8,1,128]{3,1,2,0:T(8,128)} %get-tuple-element.8), channel_id=1, source_target_pairs={{1,0},{2,1},{3,2},{4,3},{5,4},{6,5},{7,6},{0,7},{9,8},{10,9},{11,1... | collective-permute-start | bytes 417800 | tf_op jit(solution)/shard_map/ppermute | solution.py:22
  244.4 0.8 copy.12
  245.2 2.7 %gather_fusion.2 = f32[512,32,8]{1,2,0:T(8,128)} fusion(f32[32,8,512]{0,1,2:T(8,128)S(1)} %copy.12, s32[1024]{0:T(1024)S(1)} %pad_clamp_fusion), kind=kCustom, calls=%fused_computation.2 | custom fusion | bytes 1050624 | tf_op jit(solution)/shard_map/jit(_take)/gather | solution.py:44
  247.9 2.4 copy.13
  250.3 0.0 collective-permute-done
  250.4 0.0 collective-permute-done.1
  250.4 0.1 pad_maximum_fusion
  250.4 0.2 fusion.3
  250.6 0.3 fusion.6
  250.9 1.0 fusion.11
  (7 shorter events, 0.1 us)
Async XLA Ops:
  6.5 0.7 copy-start.2
  6.5 156.2 %all-gather.2.cloned.1.call-start = ((), (), s32[]{:S(2)}) async-start(), calls=%async_computation | async-start | bytes 18874368 | tf_op jit(solution)/shard_map/all_gather | solution.py:62
  7.5 9.6 %slice-start = ((bf16[8,512,1024]{2,1,0:T(8,128)(2,1)}), bf16[8,512,32]{2,1,0:T(8,128)(2,1)S(1)}, s32[]{:S(2)}) async-start(bf16[8,512,1024]{2,1,0:T(8,128)(2,1)} %param.5), calls=%async_computation.1 | async-start | bytes 2097152 | tf_op jit(solution)/shard_map/slice | solution.py:57
  7.5 10.8 %copy-start.3 = (f32[8]{0:T(128)S(1)}, f32[8]{0:T(128)}, u32[]{:S(2)}) copy-start(f32[8]{0:T(128)} %param.9) | copy-start | bytes 100
  7.5 10.8 %copy-start.1 = (s32[512]{0:T(512)S(1)}, s32[512]{0:T(512)}, u32[]{:S(2)}) copy-start(s32[512]{0:T(512)} %param.8) | copy-start | bytes 6148
  188.6 37.4 %copy-start = (f32[1024,2,512]{0,2,1:T(8,128)S(1)}, f32[1024,2,512]{0,2,1:T(8,128)}, u32[]{:S(2)}) copy-start(f32[1024,2,512]{0,2,1:T(8,128)} %convert_bitcast_fusion) | copy-start | bytes 12582916
  240.8 9.6 %collective-permute-start = (f32[34,8,1,128]{3,1,2,0:T(8,128)}, f32[34,8,1,128]{3,1,2,0:T(8,128)S(1)}, u32[]{:S(2)}, u32[]{:S(2)}) collective-permute-start(f32[34,8,1,128]{3,1,2,0:T(8,128)} %get-tuple-element.9), channel_id=1, source_target_pairs={{0,1},{1,2},{2,3},{3,4},{4,5},{5,6},{6,7},{7,0},{8,9},{9,10},{10,1... | collective-permute-start | bytes 417800 | tf_op jit(solution)/shard_map/ppermute | solution.py:20
  240.8 9.6 %collective-permute-start.1 = (f32[34,8,1,128]{3,1,2,0:T(8,128)}, f32[34,8,1,128]{3,1,2,0:T(8,128)S(1)}, u32[]{:S(2)}, u32[]{:S(2)}) collective-permute-start(f32[34,8,1,128]{3,1,2,0:T(8,128)} %get-tuple-element.8), channel_id=1, source_target_pairs={{1,0},{2,1},{3,2},{4,3},{5,4},{6,5},{7,6},{0,7},{9,8},{10,9},{11,1... | collective-permute-start | bytes 417800 | tf_op jit(solution)/shard_map/ppermute | solution.py:22
Sparse Core Ops, SparseCore 0:
  8.9 153.7 all-gather.1
where the time goes:
time: 259 us
  waiting for transfers between devices  143 us (55%)
  local copies, waits for them, and re-layouts  55.1 us (21%)
  matrix products  27.3 us (11%)
  between operations  13.6 us (5%)
  blocking collectives  8.42 us (3%)
  other arithmetic  8.19 us (3%)
  starting transfers between devices  3.55 us (1%)
    all_gather x1, waiting for transfers between devices, local(): piece = lax.all_gather(tensor, 'brick', axis=1, tiled=True)  142 us
    unnamed x10, local copies, waits for them, and re-layouts  38.7 us
    dot_general x1, matrix products, local(): lax.dot_general(piece.reshape(local_modes * rows_here, width), right_flat...  25.8 us
    all_gather x1, blocking collectives, local(): pair_all = lax.all_gather(collide, 'grp', axis=0, tiled=True)  8.42 us
    gather x1, local copies, waits for them, and re-layouts, local(): right_flat = coeffs[pairs[:, 1]].reshape(pair_count * cells, width)  5.46 us
  transfers between devices with their start and end apart: 3, of which 1 were waited for; matrix products, arithmetic and copies ran while one was open for 8% of the time, Pallas kernels for 0%

commit v1 on v0

--- a/solution.py
+++ b/solution.py
@@ -2,6 +2,7 @@
 import jax.numpy as jnp
 from jax import lax
 from jax.sharding import PartitionSpec as P
+from jax.lax import all_gather
 
 PLANE = 128
 collision_update = 0.5
@@ -59,7 +60,7 @@
     indicator_matrix = (
         pairs[:, 0][:, None] == jnp.arange(species, dtype=jnp.int32)[None, :]
     ).astype(jnp.float32)
-    piece = lax.all_gather(tensor, "brick", axis=1, tiled=True)
+    piece = jnp.concatenate(all_gather(tensor, "brick"), axis=1)
     rows_here = piece.shape[1]
     inner = lax.dot_general(
         piece.reshape(local_modes * rows_here, width),

time: 259 us -> 272 us (1.050)
  local copies, waits for them, and re-layouts: 55.1 us -> 69.1 us
    reshape x0 -> x1, local copies, waits for them, and re-layouts: none -> 14 us  [local(): piece = jnp.concatenate(all_gather(tensor, 'brick'), axis=1)]
    unnamed x10 -> x12, local copies, waits for them, and re-layouts: 38.7 us -> 38.7 us
  transfers between devices with their start and end apart: 3 -> 3, of which waited for: 1 -> 1; matrix products, arithmetic and copies ran while one was open for 8% -> 7% of each run, Pallas kernels for 0% -> 0%
where the time goes in v1:
time: 272 us
  waiting for transfers between devices  143 us (53%)
  local copies, waits for them, and re-layouts  69.1 us (25%)
  matrix products  26.6 us (10%)
  between operations  13.6 us (5%)
  blocking collectives  8.42 us (3%)
  other arithmetic  8.18 us (3%)
  starting transfers between devices  3.55 us (1%)
    all_gather x1, waiting for transfers between devices, local(): piece = jnp.concatenate(all_gather(tensor, 'brick'), axis=1)  142 us
    unnamed x12, local copies, waits for them, and re-layouts  38.7 us
    dot_general x1, matrix products, local(): lax.dot_general(piece.reshape(local_modes * rows_here, width), right_flat...  25.1 us
    reshape x1, local copies, waits for them, and re-layouts, local(): piece = jnp.concatenate(all_gather(tensor, 'brick'), axis=1)  14 us
    all_gather x1, blocking collectives, local(): pair_all = lax.all_gather(collide, 'grp', axis=0, tiled=True)  8.42 us
    gather x1, local copies, waits for them, and re-layouts, local(): right_flat = coeffs[pairs[:, 1]].reshape(pair_count * cells, width)  5.47 us
  transfers between devices with their start and end apart: 3, of which 1 were waited for; matrix products, arithmetic and copies ran while one was open for 7% of the time, Pallas kernels for 0%

profile of v1, /device:TPU:0, one launch (start us, length us, event | category | flops | bytes accessed | tf_op | source)
XLA Modules:
  0.0 272.0 jit_solution(11393871451394540053)
XLA Ops:
  6.5 0.0 copy-start.3
  6.5 0.0 all-gather.3.cloned.1.call-start
  6.5 0.7 all-gather.3.cloned.1.call-update
  7.3 0.0 copy-done.3
  7.3 0.2 slice_reduce_fusion
  7.5 0.0 slice-start
  7.5 0.0 copy-start.4
  7.5 0.0 copy-start.2
  7.5 5.5 %gather_fusion = bf16[2,512,1024]{2,1,0:T(8,128)(2,1)} fusion(bf16[8,512,1024]{2,1,0:T(8,128)(2,1)} %param.5, s32[1024]{0:T(1024)S(1)} %get-tuple-element.11), kind=kCustom, calls=%fused_computation | custom fusion | bytes 4194312 | tf_op jit(solution)/shard_map/gather | solution.py:57
  13.0 4.1 %gather_fusion.1 = bf16[2,512,1024]{2,1,0:T(8,128)(2,1)S(1)} fusion(bf16[8,512,1024]{2,1,0:T(8,128)(2,1)} %param.5, s32[1024]{0:T(1024)S(1)} %get-tuple-element.10), kind=kCustom, calls=%fused_computation.1 | custom fusion | bytes 4194312 | tf_op jit(solution)/shard_map/gather | solution.py:56
  17.0 0.0 slice-done
  17.0 1.2 copy.19
  18.3 0.0 copy-done.4
  18.3 0.0 copy-done.2
  18.3 2.6 convert_bitcast_fusion
  20.9 141.9 %all-gather.3.cloned.1.call-done = bf16[64,128,1024]{2,1,0:T(8,128)(2,1)} async-done(((bf16[8,128,1024]{2,1,0:T(8,128)(2,1)}), bf16[64,128,1024]{2,1,0:T(8,128)(2,1)}) %all-gather.3.cloned.1.call-update) | async-done | bytes 16777232 | tf_op jit(solution)/shard_map/all_gather | solution.py:63
  162.8 0.0 copy-start.1
  162.8 14.0 %copy.15 = bf16[8,8,128,1024]{3,2,1,0:T(8,128)(2,1)} copy(bf16[8,8,128,1024]{3,2,0,1:T(8,128)(2,1)} %bitcast.38) | data formatting | bytes 33554432 | tf_op jit(solution)/shard_map/reshape | solution.py:63
  176.8 0.0 copy-done.1
  176.8 25.1 %fusion.22 = f32[1024,8192]{1,0:T(8,128)} fusion(bf16[1024,1024]{1,0:T(8,128)(2,1)S(1)} %bitcast.43, bf16[8192,1024]{1,0:T(8,128)(2,1)} %bitcast.39), kind=kOutput, calls=%fused_computation.47 | convolution fusion | flops 17179869184 | bytes 52428800 | tf_op jit(solution)/shard_map/dot_general | solution.py:65
  201.9 0.0 copy-start
  201.9 37.4 %copy.20 = f32[128,8,8,1024]{3,2,1,0:T(8,128)S(1)} copy(f32[128,8,8,1024]{3,1,2,0:T(8,128)} %bitcast.37) | data formatting | bytes 67108864
  239.3 0.0 copy-done
  239.3 3.9 %multiply_reduce_fusion = f32[8,2,512]{0,2,1:T(8,128)S(1)} fusion(f32[8,1024,2,512]{1,0,3,2:T(8,128)S(1)} %bitcast.36, f32[1024,2,512]{0,2,1:T(8,128)S(1)} %copy-done), kind=kLoop, calls=%fused_computation.3 | loop fusion | flops 16769024 | bytes 37781504 | tf_op jit(solution)/shard_map/reduce_sum | solution.py:73
  243.3 0.2 copy.16
  243.4 8.4 %all_gather.11 = f32[32,2,512]{2,1,0:T(2,128)S(1)} all-gather(f32[8,2,512]{2,1,0:T(2,128)S(1)} %copy.16), channel_id=1, replica_groups=mesh['grp'=4,'brick'=8] {'grp'}, dimensions={0}, use_global_device_ids=true | all-gather | bytes 163840 | tf_op jit(solution)/shard_map/all_gather | solution.py:74
  251.9 1.5 fusion.1
  253.3 0.7 fusion.21
  254.1 0.0 collective-permute-start
  254.1 3.5 %collective-permute-start.1 = (f32[34,8,1,128]{3,1,2,0:T(8,128)}, f32[34,8,1,128]{3,1,2,0:T(8,128)S(1)}, u32[]{:S(2)}, u32[]{:S(2)}) collective-permute-start(f32[34,8,1,128]{3,1,2,0:T(8,128)} %get-tuple-element.8), channel_id=1, source_target_pairs={{1,0},{2,1},{3,2},{4,3},{5,4},{6,5},{7,6},{0,7},{9,8},{10,9},{11,1... | collective-permute-start | bytes 417800 | tf_op jit(solution)/shard_map/ppermute | solution.py:23
  257.7 0.8 copy.17
  258.5 2.7 %gather_fusion.2 = f32[512,32,8]{1,2,0:T(8,128)} fusion(f32[32,8,512]{0,1,2:T(8,128)S(1)} %copy.17, s32[1024]{0:T(1024)S(1)} %pad_clamp_fusion), kind=kCustom, calls=%fused_computation.2 | custom fusion | bytes 1050624 | tf_op jit(solution)/shard_map/jit(_take)/gather | solution.py:45
  261.2 2.4 copy.18
  263.6 0.0 collective-permute-done
  263.7 0.0 collective-permute-done.1
  263.7 0.1 pad_maximum_fusion
  263.7 0.2 fusion.3
  263.9 0.3 fusion.6
  264.2 1.0 fusion.11
  (7 shorter events, 0.1 us)
Async XLA Ops:
  6.5 0.7 copy-start.3
  6.5 156.2 %all-gather.3.cloned.1.call-start = ((), (), s32[]{:S(2)}) async-start(), calls=%async_computation | async-start | bytes 18874368 | tf_op jit(solution)/shard_map/all_gather | solution.py:63
  7.5 9.6 %slice-start = ((bf16[8,512,1024]{2,1,0:T(8,128)(2,1)}), bf16[8,512,32]{2,1,0:T(8,128)(2,1)S(1)}, s32[]{:S(2)}) async-start(bf16[8,512,1024]{2,1,0:T(8,128)(2,1)} %param.5), calls=%async_computation.1 | async-start | bytes 2097152 | tf_op jit(solution)/shard_map/slice | solution.py:58
  7.5 10.8 %copy-start.4 = (f32[8]{0:T(128)S(1)}, f32[8]{0:T(128)}, u32[]{:S(2)}) copy-start(f32[8]{0:T(128)} %param.9) | copy-start | bytes 100
  7.5 10.8 %copy-start.2 = (s32[512]{0:T(512)S(1)}, s32[512]{0:T(512)}, u32[]{:S(2)}) copy-start(s32[512]{0:T(512)} %param.8) | copy-start | bytes 6148
  162.8 14.0 %copy-start.1 = (bf16[2,512,1024]{2,1,0:T(8,128)(2,1)S(1)}, bf16[2,512,1024]{2,1,0:T(8,128)(2,1)}, u32[]{:S(2)}) copy-start(bf16[2,512,1024]{2,1,0:T(8,128)(2,1)} %gather_fusion) | copy-start | bytes 6291460
  201.9 37.4 %copy-start = (f32[1024,2,512]{0,2,1:T(8,128)S(1)}, f32[1024,2,512]{0,2,1:T(8,128)}, u32[]{:S(2)}) copy-start(f32[1024,2,512]{0,2,1:T(8,128)} %convert_bitcast_fusion) | copy-start | bytes 12582916
  254.1 9.6 %collective-permute-start = (f32[34,8,1,128]{3,1,2,0:T(8,128)}, f32[34,8,1,128]{3,1,2,0:T(8,128)S(1)}, u32[]{:S(2)}, u32[]{:S(2)}) collective-permute-start(f32[34,8,1,128]{3,1,2,0:T(8,128)} %get-tuple-element.9), channel_id=1, source_target_pairs={{0,1},{1,2},{2,3},{3,4},{4,5},{5,6},{6,7},{7,0},{8,9},{9,10},{10,1... | collective-permute-start | bytes 417800 | tf_op jit(solution)/shard_map/ppermute | solution.py:21
  254.1 9.6 %collective-permute-start.1 = (f32[34,8,1,128]{3,1,2,0:T(8,128)}, f32[34,8,1,128]{3,1,2,0:T(8,128)S(1)}, u32[]{:S(2)}, u32[]{:S(2)}) collective-permute-start(f32[34,8,1,128]{3,1,2,0:T(8,128)} %get-tuple-element.8), channel_id=1, source_target_pairs={{1,0},{2,1},{3,2},{4,3},{5,4},{6,5},{7,6},{0,7},{9,8},{10,9},{11,1... | collective-permute-start | bytes 417800 | tf_op jit(solution)/shard_map/ppermute | solution.py:23
Sparse Core Ops, SparseCore 0:
  8.9 153.7 all-gather.2
